TPU v7x, 32 devices: a whole 2x2x4 slice. The times are simulated.
32 devices in a mesh: src: 4 (over x, core), gauge: 8 (over z, y).
Axes of the slice: x: 2, y: 2, z: 4, core: 2. Of those that a mesh axis runs over, the one named last changes fastest.
Arguments:
- green: bfloat16 [128, 512, 4096], P('gauge', None, 'src'), may hold values from -0.234375 to 0.234375
- observed: float32 [128, 128, 512], P(None, 'gauge'), may hold values from -8 to 8
- gauge_mask: int32 [128], P('gauge'), may hold values 0 or 1
- source_mask: int32 [4096], P('src'), may hold values 0 or 1
Outputs:
- slip: float32 [128, 4096], P(None, 'src')
- residual: float32 [128, 128, 512], P(None, 'gauge')
All inputs are finite; a program needn't handle non-finite values. No bound on the sum of `gauge_mask` or of `source_mask` on one device may be relied on, other than what follows from the above.
Results may differ from a plain program's by a relative error of at most 0.023.
Values may be sent and summed in bfloat16 or wider, within the bound.
A program may use at most 64 MiB of HBM per device.

v0:
```python
import jax
import jax.numpy as jnp
from jax import lax
from jax.sharding import PartitionSpec as P

ITERS = 3


def project(vector, green):
    return lax.dot_general(
        vector, green, (((1,), (2,)), ((), ())), preferred_element_type=jnp.float32
    )


def gradient(green, wave, ps_local):
    part = lax.dot_general(
        wave.astype(jnp.bfloat16),
        green,
        (((1, 2), (0, 1)), ((), ())),
        preferred_element_type=jnp.float32,
    )
    grad = ps_local * lax.psum(part.astype(jnp.bfloat16), "gauge").astype(jnp.float32)
    gamma = lax.psum(jnp.sum(grad * grad, axis=1), "src")
    return (grad, gamma)


def per_device(green, observed, gauge_mask, source_mask):
    wg = gauge_mask.astype(jnp.float32)[None, :, None]
    ps_local = source_mask.astype(jnp.float32)[None, :]
    residual = wg * observed
    events = observed.shape[0]
    slip = jnp.zeros((events, green.shape[2]), jnp.float32)
    grad, gamma = gradient(green, residual, ps_local)
    direction = grad
    for step in range(ITERS):
        direction_bf = direction.astype(jnp.bfloat16)
        rows = events // lax.axis_size("src")
        offset = lax.axis_index("src") * rows
        predicted = wg * lax.psum_scatter(
            project(direction_bf, green).astype(jnp.bfloat16),
            "src",
            scatter_dimension=0,
            tiled=True,
        ).astype(jnp.float32)
        curvature = lax.psum(jnp.sum(predicted * predicted, axis=(1, 2)), "gauge")
        alpha_rows = lax.dynamic_slice_in_dim(gamma, offset, rows, 0) / curvature
        kept = (
            lax.dynamic_slice_in_dim(residual, offset, rows, 0)
            - alpha_rows[:, None, None] * predicted
        )
        residual, alpha = (
            lax.all_gather(kept.astype(jnp.bfloat16), "src", axis=0, tiled=True).astype(kept.dtype),
            lax.all_gather(alpha_rows.astype(jnp.bfloat16), "src", axis=0, tiled=True).astype(
                alpha_rows.dtype
            ),
        )
        slip = slip + alpha[:, None] * direction
        if step + 1 < ITERS:
            grad, fresh = gradient(green, residual, ps_local)
            direction = grad + (fresh / gamma)[:, None] * direction
            gamma = fresh
    return (slip, residual)


def solution(mesh):
    return jax.shard_map(
        per_device,
        mesh=mesh,
        in_specs=(P("gauge", None, "src"), P(None, "gauge", None), P("gauge"), P("src")),
        out_specs=(P(None, "src"), P(None, "gauge", None)),
        check_vma=False,
    )
```

profile of v0, /device:TPU:0, one launch (start us, length us, event | category | flops | bytes accessed | tf_op | source)
XLA Modules:
  0.0 548.1 jit_solution(5217770107411388687)
XLA Ops:
  7.2 0.0 all-reduce.8.cloned.1.call-start
  7.2 0.7 convert_element_type.93
  7.9 4.6 copy_multiply_fusion
  12.5 0.0 copy-start
  12.5 2.0 copy-done
  14.5 9.1 %fusion.7 = bf16[128,1024]{1,0:T(8,128)(2,1)} fusion(bf16[16,512,1024]{2,1,0:T(8,128)(2,1)} %param.4, f32[128,16,512]{2,0,1:T(8,128)S(1)} %copy_multiply_fusion), kind=kOutput, calls=%fused_computation.11 | convolution fusion | flops 2148663296 | bytes 21233664 | tf_op jit(solution)/shard_map/dot_general | solution.py:16
  23.6 0.0 all-reduce.8.cloned.1.call-update
  23.6 0.0 reduce-scatter.4.cloned.1.call-start
  23.7 73.8 %all-reduce.8.cloned.1.call-done = bf16[128,1024]{1,0:T(8,128)(2,1)} async-done(((bf16[128,1024]{1,0:T(8,128)(2,1)}), bf16[128,1024]{1,0:T(8,128)(2,1)}) %all-reduce.8.cloned.1.call-update) | async-done | bytes 262160 | tf_op jit(solution)/shard_map/psum | solution.py:22
  97.5 12.9 %convolution_convert_fusion.2 = bf16[128,16,512]{2,0,1:T(8,128)(2,1)} fusion(bf16[16,512,1024]{2,1,0:T(8,128)(2,1)} %param.4, bf16[128,1024]{1,0:T(8,128)(2,1)} %all-reduce.8.cloned.1.call-done, f32[1024]{0:T(1024)S(1)} %convert_element_type.92), kind=kOutput, calls=%fused_computation.5 | convolution fusion | flops 2148925440 | bytes 19140608 | tf_op jit(solution)/shard_map/dot_general | solution.py:10
  110.4 0.0 reduce-scatter.4.cloned.1.call-update
  110.4 0.0 all-gather.4.cloned.1.call-start
  110.4 0.2 multiply_reduce_fusion.5
  110.6 5.7 %psum.64 = f32[128]{0:T(128)S(1)} all-reduce(f32[128]{0:T(128)S(1)} %multiply_reduce_fusion.5), channel_id=1, replica_groups=mesh['src'=4,'gauge'=8] {'src'}, use_global_device_ids=true, to_apply=%region_2.0 | all-reduce | flops 128 | bytes 1024 | tf_op jit(solution)/shard_map/psum | solution.py:23
  116.3 24.6 %reduce-scatter.4.cloned.1.call-done = bf16[32,16,512]{2,0,1:T(8,128)(2,1)} async-done(((bf16[128,16,512]{2,0,1:T(8,128)(2,1)}), bf16[32,16,512]{2,0,1:T(8,128)(2,1)}) %reduce-scatter.4.cloned.1.call-update) | async-done | bytes 524304 | tf_op jit(solution)/shard_map/reduce_scatter | solution.py:39
  140.9 1.3 multiply_reduce_fusion.2
  142.2 21.4 %psum.65 = f32[32]{0:T(128)S(1)} all-reduce(f32[32]{0:T(128)S(1)} %multiply_reduce_fusion.2), channel_id=1, replica_groups=mesh['src'=4,'gauge'=8] {'gauge'}, use_global_device_ids=true, to_apply=%region_5.0 | all-reduce | flops 32 | bytes 256 | tf_op jit(solution)/shard_map/psum | solution.py:45
  163.6 0.1 fusion.25
  163.7 2.5 subtract_convert_fusion.2
  166.2 0.0 all-gather.4.cloned.1.call-update
  166.3 0.2 all-reduce.10.cloned.1.call-start
  166.5 18.8 %all-gather.4.cloned.1.call-done = bf16[128,16,512]{2,0,1:T(8,128)(2,1)} async-done(((bf16[32,16,512]{2,0,1:T(8,128)(2,1)}), bf16[128,16,512]{2,0,1:T(8,128)(2,1)}) %all-gather.4.cloned.1.call-update) | async-done | bytes 2097168 | tf_op jit(solution)/shard_map/all_gather | solution.py:52
  185.3 9.4 %fusion.5 = bf16[128,1024]{1,0:T(8,128)(2,1)} fusion(bf16[128,16,512]{2,0,1:T(8,128)(2,1)} %all-gather.4.cloned.1.call-done, bf16[16,512,1024]{2,1,0:T(8,128)(2,1)} %param.4), kind=kOutput, calls=%fused_computation.9 | convolution fusion | flops 2147614720 | bytes 19136512 | tf_op jit(solution)/shard_map/dot_general | solution.py:16
  194.8 0.0 all-reduce.10.cloned.1.call-update
  194.8 0.0 reduce-scatter.6.cloned.1.call-start
  194.8 71.1 %all-reduce.10.cloned.1.call-done = bf16[128,1024]{1,0:T(8,128)(2,1)} async-done(((bf16[128,1024]{1,0:T(8,128)(2,1)}), bf16[128,1024]{1,0:T(8,128)(2,1)}) %all-reduce.10.cloned.1.call-update) | async-done | bytes 262160 | tf_op jit(solution)/shard_map/psum | solution.py:22
  265.9 1.1 multiply_reduce_fusion.4
  267.0 5.7 %psum.67 = f32[128]{0:T(128)S(1)} all-reduce(f32[128]{0:T(128)S(1)} %multiply_reduce_fusion.4), channel_id=1, replica_groups=mesh['src'=4,'gauge'=8] {'src'}, use_global_device_ids=true, to_apply=%region_8.0 | all-reduce | flops 128 | bytes 1024 | tf_op jit(solution)/shard_map/psum | solution.py:23
  272.7 12.9 %convolution_convert_fusion.1 = bf16[128,16,512]{2,0,1:T(8,128)(2,1)} fusion(bf16[16,512,1024]{2,1,0:T(8,128)(2,1)} %param.4, bf16[128,1024]{1,0:T(8,128)(2,1)S(1)} %copy-done.1, bf16[128,1024]{1,0:T(8,128)(2,1)} %all-reduce.10.cloned.1.call-done, f32[128]{0:T(128)S(1)} %div.16, f32[1024]{0:T(1024)S(1)} %convert_element_type.92), kind=kOutput, calls=%fused_computation.4 | convolution fusion | flops 2149449728 | bytes 19403264 | tf_op jit(solution)/shard_map/dot_general | solution.py:10
  285.6 0.0 reduce-scatter.6.cloned.1.call-update
  285.6 0.0 all-gather.6.cloned.1.call-start
  285.7 30.7 %reduce-scatter.6.cloned.1.call-done = bf16[32,16,512]{2,0,1:T(8,128)(2,1)} async-done(((bf16[128,16,512]{2,0,1:T(8,128)(2,1)}), bf16[32,16,512]{2,0,1:T(8,128)(2,1)}) %reduce-scatter.6.cloned.1.call-update) | async-done | bytes 524304 | tf_op jit(solution)/shard_map/reduce_scatter | solution.py:39
  316.4 1.3 multiply_reduce_fusion.1
  317.7 21.4 %psum.68 = f32[32]{0:T(128)S(1)} all-reduce(f32[32]{0:T(128)S(1)} %multiply_reduce_fusion.1), channel_id=1, replica_groups=mesh['src'=4,'gauge'=8] {'gauge'}, use_global_device_ids=true, to_apply=%region_11.0 | all-reduce | flops 32 | bytes 256 | tf_op jit(solution)/shard_map/psum | solution.py:45
  339.1 0.1 fusion.26
  339.2 2.6 subtract_convert_fusion.1
  341.8 0.0 all-gather.6.cloned.1.call-update
  341.8 0.0 copy-start.2
  341.8 0.0 all-reduce.12.cloned.1.call-start
  341.9 19.0 %all-gather.6.cloned.1.call-done = bf16[128,16,512]{2,0,1:T(8,128)(2,1)} async-done(((bf16[32,16,512]{2,0,1:T(8,128)(2,1)}), bf16[128,16,512]{2,0,1:T(8,128)(2,1)}) %all-gather.6.cloned.1.call-update) | async-done | bytes 2097168 | tf_op jit(solution)/shard_map/all_gather | solution.py:52
  360.9 9.4 %fusion.6 = bf16[128,1024]{1,0:T(8,128)(2,1)} fusion(bf16[128,16,512]{2,0,1:T(8,128)(2,1)} %all-gather.6.cloned.1.call-done, bf16[16,512,1024]{2,1,0:T(8,128)(2,1)} %param.4), kind=kOutput, calls=%fused_computation.10 | convolution fusion | flops 2147614720 | bytes 19136512 | tf_op jit(solution)/shard_map/dot_general | solution.py:16
  370.3 0.0 all-reduce.12.cloned.1.call-update
  370.3 0.0 reduce-scatter.8.cloned.1.call-start
  370.4 71.1 %all-reduce.12.cloned.1.call-done = bf16[128,1024]{1,0:T(8,128)(2,1)} async-done(((bf16[128,1024]{1,0:T(8,128)(2,1)}), bf16[128,1024]{1,0:T(8,128)(2,1)}) %all-reduce.12.cloned.1.call-update) | async-done | bytes 262160 | tf_op jit(solution)/shard_map/psum | solution.py:22
  441.5 1.1 multiply_reduce_fusion.3
  442.6 5.9 %psum.70 = f32[128]{0:T(128)S(1)} all-reduce(f32[128]{0:T(128)S(1)} %multiply_reduce_fusion.3), channel_id=1, replica_groups=mesh['src'=4,'gauge'=8] {'src'}, use_global_device_ids=true, to_apply=%region_14.0 | all-reduce | flops 128 | bytes 1024 | tf_op jit(solution)/shard_map/psum | solution.py:23
  448.5 12.9 %convolution_convert_fusion = bf16[128,16,512]{2,0,1:T(8,128)(2,1)} fusion(bf16[16,512,1024]{2,1,0:T(8,128)(2,1)} %param.4, bf16[128,1024]{1,0:T(8,128)(2,1)S(1)} %copy-done.1, bf16[128,1024]{1,0:T(8,128)(2,1)S(1)} %copy-done.2, bf16[128,1024]{1,0:T(8,128)(2,1)} %all-reduce.12.cloned.1.call-done, f32[128]{0:T(128)S(1)} %div.18, f32[128]{0:T(128)S(1)} %div.16, ...), kind=kOutput, calls=%fused_computation.3 | convolution fusion | flops 2149974016 | bytes 19665920 | tf_op jit(solution)/shard_map/dot_general | solution.py:10
  461.4 0.0 reduce-scatter.8.cloned.1.call-update
  461.4 0.0 all-gather.8.cloned.1.call-start
  461.5 30.7 %reduce-scatter.8.cloned.1.call-done = bf16[32,16,512]{2,0,1:T(8,128)(2,1)} async-done(((bf16[128,16,512]{2,0,1:T(8,128)(2,1)}), bf16[32,16,512]{2,0,1:T(8,128)(2,1)}) %reduce-scatter.8.cloned.1.call-update) | async-done | bytes 524304 | tf_op jit(solution)/shard_map/reduce_scatter | solution.py:39
  492.2 1.3 multiply_reduce_fusion
  493.6 21.4 %psum.71 = f32[32]{0:T(128)S(1)} all-reduce(f32[32]{0:T(128)S(1)} %multiply_reduce_fusion), channel_id=1, replica_groups=mesh['src'=4,'gauge'=8] {'gauge'}, use_global_device_ids=true, to_apply=%region_17.0 | all-reduce | flops 32 | bytes 256 | tf_op jit(solution)/shard_map/psum | solution.py:45
  514.9 0.1 fusion.27
  515.0 2.6 subtract_convert_fusion
  517.6 0.0 all-gather.8.cloned.1.call-update
  517.7 0.6 dynamic-slice
  518.9 0.2 dynamic-update-slice
  519.2 0.2 dynamic-update-slice.1
  519.4 0.2 dynamic-update-slice.2
  519.6 6.0 %all-reduce.3 = (bf16[128]{0:T(256)(128)(2,1)S(1)}, bf16[128]{0:T(256)(128)(2,1)S(1)}, bf16[128]{0:T(256)(128)(2,1)S(1)}) all-reduce(bf16[128]{0:T(256)(128)(2,1)S(1)} %dynamic-update-slice.2, bf16[128]{0:T(256)(128)(2,1)S(1)} %dynamic-update-slice.1, bf16[128]{0:T(256)(128)(2,1)S(1)} %dynamic-update-slice), channel_id=1, replica_groups=mesh['src'=4,'gauge'=8] {'src'}, use_global_device_ids=true, to_apply=%add.2 | all-reduce | flops 384 | bytes 1536
  525.7 0.0 copy-done.3
  525.7 1.1 multiply_add_fusion
  526.8 9.9 %all-gather.8.cloned.1.call-done = bf16[128,16,512]{2,0,1:T(8,128)(2,1)} async-done(((bf16[32,16,512]{2,0,1:T(8,128)(2,1)}), bf16[128,16,512]{2,0,1:T(8,128)(2,1)}) %all-gather.8.cloned.1.call-update) | async-done | bytes 2097168 | tf_op jit(solution)/shard_map/all_gather | solution.py:52
  536.7 4.8 copy.7
  (17 shorter events, 0.1 us)
Async XLA Ops:
  7.2 90.3 %all-reduce.8.cloned.1.call-start = ((), (), s32[]{:S(2)}) async-start(), calls=%async_computation.3 | async-start | bytes 524288 | tf_op jit(solution)/shard_map/psum | solution.py:22
  12.5 2.0 copy-start
  14.5 9.2 %copy-start.4 = (s32[1024]{0:T(1024)S(1)}, s32[1024]{0:T(1024)}, u32[]{:S(2)}) copy-start(s32[1024]{0:T(1024)} %param.7) | copy-start | bytes 12292
  23.6 117.3 %reduce-scatter.4.cloned.1.call-start = ((), (), s32[]{:S(2)}) async-start(), calls=%async_computation.4 | async-start | bytes 2621440 | tf_op jit(solution)/shard_map/reduce_scatter | solution.py:39
  97.5 13.0 %copy-start.1 = (bf16[128,1024]{1,0:T(8,128)(2,1)S(1)}, bf16[128,1024]{1,0:T(8,128)(2,1)}, u32[]{:S(2)}) copy-start(bf16[128,1024]{1,0:T(8,128)(2,1)} %all-reduce.8.cloned.1.call-done) | copy-start | bytes 786436
  110.4 74.9 %all-gather.4.cloned.1.call-start = ((), (), s32[]{:S(2)}) async-start(), calls=%async_computation.5 | async-start | bytes 2621440 | tf_op jit(solution)/shard_map/all_gather | solution.py:52
  166.3 99.7 %all-reduce.10.cloned.1.call-start = ((), (), s32[]{:S(2)}) async-start(), calls=%async_computation.6 | async-start | bytes 524288 | tf_op jit(solution)/shard_map/psum | solution.py:22
  194.8 121.6 %reduce-scatter.6.cloned.1.call-start = ((), (), s32[]{:S(2)}) async-start(), calls=%async_computation.7 | async-start | bytes 2621440 | tf_op jit(solution)/shard_map/reduce_scatter | solution.py:39
  285.6 75.3 %all-gather.6.cloned.1.call-start = ((), (), s32[]{:S(2)}) async-start(), calls=%async_computation.8 | async-start | bytes 2621440 | tf_op jit(solution)/shard_map/all_gather | solution.py:52
  341.8 106.7 %copy-start.2 = (bf16[128,1024]{1,0:T(8,128)(2,1)S(1)}, bf16[128,1024]{1,0:T(8,128)(2,1)}, u32[]{:S(2)}) copy-start(bf16[128,1024]{1,0:T(8,128)(2,1)} %all-reduce.10.cloned.1.call-done) | copy-start | bytes 786436
  341.8 99.7 %all-reduce.12.cloned.1.call-start = ((), (), s32[]{:S(2)}) async-start(), calls=%async_computation.9 | async-start | bytes 524288 | tf_op jit(solution)/shard_map/psum | solution.py:22
  370.3 121.9 %reduce-scatter.8.cloned.1.call-start = ((), (), s32[]{:S(2)}) async-start(), calls=%async_computation.10 | async-start | bytes 2621440 | tf_op jit(solution)/shard_map/reduce_scatter | solution.py:39
  461.4 56.3 %copy-start.5 = (u32[32]{0:T(128)S(1)}, u32[32]{0:T(128)}, u32[]{:S(2)}) copy-start(u32[32]{0:T(128)} %constant.15) | copy-start | bytes 388
  461.4 64.3 %copy-start.3 = (bf16[128,1024]{1,0:T(8,128)(2,1)S(1)}, bf16[128,1024]{1,0:T(8,128)(2,1)}, u32[]{:S(2)}) copy-start(bf16[128,1024]{1,0:T(8,128)(2,1)} %all-reduce.12.cloned.1.call-done) | copy-start | bytes 786436
  461.4 75.3 %all-gather.8.cloned.1.call-start = ((), (), s32[]{:S(2)}) async-start(), calls=%async_computation.11 | async-start | bytes 2621440 | tf_op jit(solution)/shard_map/all_gather | solution.py:52
Sparse Core Ops, SparseCore 0:
  23.7 73.6 all-reduce.7
  110.5 30.3 reduce-scatter.3
  166.4 18.8 all-gather.3
  194.9 70.9 all-reduce.9
  285.7 30.6 reduce-scatter.5
  341.9 18.8 all-gather.5
  370.5 70.9 all-reduce.11
  461.6 30.6 reduce-scatter.7
  517.8 18.9 all-gather.7
where the time goes:
time: 549 us; the launch traced here: 548 us
  waiting for transfers between devices  350 us (64%)
  blocking collectives  87.3 us (16%)
  matrix products  66.6 us (12%)
  other arithmetic  20.9 us (4%)
  between operations  14.6 us (3%)
  local copies, waits for them, and re-layouts  8.12 us (1%)
    psum x3, waiting for transfers between devices, gradient(): lax.psum(part.astype(jnp.bfloat16), 'gauge').astype(jnp.float32)  216 us
    reduce_scatter x3, waiting for transfers between devices, per_device(): lax.psum_scatter(project(direction_bf, green).astype(jnp.bfloat16), 'src'...  86.1 us
    psum x3, blocking collectives, per_device(): curvature = lax.psum(jnp.sum(predicted * predicted, axis=(1, 2)), 'gauge')  64.1 us
    all_gather x3, waiting for transfers between devices, per_device(): lax.all_gather(kept.astype(jnp.bfloat16), 'src', axis=0, tiled=True)  47.8 us
    dot_general x3, matrix products, project(): lax.dot_general(vector, green, (((1,), (2,)), ((), ())), preferred_elemen...  38.7 us
    dot_general x3, matrix products, gradient(): lax.dot_general(wave.astype(jnp.bfloat16), green, (((1, 2), (0, 1)), ((),...  28 us
    psum x3, blocking collectives, gradient(): gamma = lax.psum(jnp.sum(grad * grad, axis=1), 'src')  17.2 us
  transfers between devices with their start and end apart: 9, of which 9 were waited for; matrix products, arithmetic and copies ran while one was open for 0% of the time, Pallas kernels for 0%

commit v1 on v0

v1 whole, which is shorter than its diff:
```python
import functools

import jax
import jax.numpy as jnp
from jax import lax
from jax.experimental import pallas as pl
from jax.experimental.pallas import tpu as pltpu
from jax.sharding import PartitionSpec as P

ITERS = 3
GROUPS = 2
PAIR = 2
LAG = 2
LANES = 128
MESH = pl.DeviceIdType.MESH
F32 = jnp.float32
BF16 = jnp.bfloat16


def cg_kernel(
    peers, src_size, gpc,
    green_hbm, obs_ref, wg_ref, ps_ref,
    slip_ref, res_ref,
    green, part, r1, xs, xr, u, v, grad, gbf, dirn, vdir, csum, coef,
    gs, gr, ag, aq, cr, ca, cq, gm, gmr,
    green_sem, s1_send, s1_recv, x_send, x_recv, u_send, u_recv,
    rs_send, rs_recv, ag_send, ag_recv, cs_send, cs_recv, ca_send, ca_recv, gm_send, gm_recv,
):
    gauges, times, width = green.shape
    events = v.shape[0]
    eg = events // GROUPS
    half = eg // 2
    own = eg // peers
    chunks = gauges // gpc
    src = lax.axis_index("src")
    me = lax.axis_index("gauge")
    core = src % PAIR
    chip = src // PAIR
    sib = chip * PAIR + (1 - core)
    across = (1 - chip) * PAIR + core

    def green_copy(g):
        return pltpu.make_async_copy(green_hbm.at[g], green.at[g], green_sem.at[g])

    def start_green(g, _):
        green_copy(g).start()
        return 0

    lax.fori_loop(0, gauges, start_green, 0)

    barrier = pltpu.get_barrier_semaphore()
    for d in range(1, peers):
        pl.semaphore_signal(barrier, inc=1, device_id={"gauge": (me + d) % peers}, device_id_type=MESH)
    for d in range(1, src_size):
        pl.semaphore_signal(barrier, inc=1, device_id={"src": (src + d) % src_size}, device_id_type=MESH)
    pl.semaphore_wait(barrier, peers + src_size - 2)

    def rows(q):
        return slice(q * eg, (q + 1) * eg)

    def mine(q):
        return pl.ds(pl.multiple_of(q * eg + core * half, half), half)

    def theirs(q):
        return pl.ds(pl.multiple_of(q * eg + (1 - core) * half, half), half)

    def packed(q):
        return slice(q * half, (q + 1) * half)

    def span(c):
        return pl.ds(c * gpc, gpc)

    my_cols = pl.ds(pl.multiple_of(me * LANES, LANES), LANES)

    def rcopy(src_ref, dst_ref, send, recv, to):
        return pltpu.make_async_remote_copy(
            src_ref=src_ref, dst_ref=dst_ref, send_sem=send, recv_sem=recv,
            device_id=to, device_id_type=MESH,
        )

    def s1_copy(it, q, c):
        return rcopy(part.at[it, span(c), theirs(q)], r1.at[it, span(c), packed(q)],
                     s1_send.at[it, q, c], s1_recv.at[it, q, c], {"src": sib})

    def x_copy(it, q, c):
        return rcopy(xs.at[it, span(c), packed(q)], xr.at[it, span(c), packed(q)],
                     x_send.at[it, q, c], x_recv.at[it, q, c], {"src": across})

    def u_copy(it, q, c):
        return rcopy(u.at[it, span(c), mine(q)], u.at[it, span(c), mine(q)],
                     u_send.at[it, q, c], u_recv.at[it, q, c], {"src": sib})

    def u_arrive(it, q, c):
        return rcopy(u.at[it, span(c), theirs(q)], u.at[it, span(c), theirs(q)],
                     u_send.at[it, q, c], u_recv.at[it, q, c], {"src": sib})

    def rs_copy(k, q, d):
        p = (me + d) % peers
        cols = pl.ds(pl.multiple_of(p * LANES, LANES), LANES)
        return rcopy(gs.at[k, q, :, cols], gr.at[k, q, d - 1],
                     rs_send.at[k, q, d - 1], rs_recv.at[k, q, d - 1], {"gauge": p})

    def ag_copy(k, q, d):
        p = (me + d) % peers
        return rcopy(ag.at[k, q], aq.at[k, q, :, my_cols],
                     ag_send.at[k, q, d - 1], ag_recv.at[k, q, d - 1], {"gauge": p})

    def ag_arrive(k, q, d):
        p = (me + peers - d) % peers
        cols = pl.ds(pl.multiple_of(p * LANES, LANES), LANES)
        return rcopy(ag.at[k, q], aq.at[k, q, :, cols],
                     ag_send.at[k, q, d - 1], ag_recv.at[k, q, d - 1], {"gauge": p})

    def own_rows(p):
        return pl.ds(pl.multiple_of(p * own, own), own)

    def cs_copy(it, q, d):
        p = (me + d) % peers
        return rcopy(csum.at[it, q, own_rows(p)], cr.at[it, q, d - 1],
                     cs_send.at[it, q, d - 1], cs_recv.at[it, q, d - 1], {"gauge": p})

    def ca_copy(it, q, d):
        p = (me + d) % peers
        return rcopy(ca.at[it, q], cq.at[it, q, own_rows(me)],
                     ca_send.at[it, q, d - 1], ca_recv.at[it, q, d - 1], {"gauge": p})

    def ca_arrive(it, q, d):
        p = (me + peers - d) % peers
        return rcopy(ca.at[it, q], cq.at[it, q, own_rows(p)],
                     ca_send.at[it, q, d - 1], ca_recv.at[it, q, d - 1], {"gauge": p})

    def gm_copy(it, q, d):
        return rcopy(gm.at[it, q], gmr.at[it, q, d - 1],
                     gm_send.at[it, q, d - 1], gm_recv.at[it, q, d - 1],
                     {"src": (src + d) % src_size})

    hops = range(1, peers)

    def rs_start(k, q, with_v, it):
        if with_v:
            gs[k, q] = v[rows(q), :].astype(BF16)
        if it is not None:
            csum[it, q] = jnp.broadcast_to(
                jnp.sum(csum[it, q], axis=1, keepdims=True), (eg, LANES))
        for d in hops:
            if it is not None:
                cs_copy(it, q, d).start()
            if with_v:
                rs_copy(k, q, d).start()

    def ag_start(k, q, with_v, it):
        if it is not None:
            total = csum[it, q, own_rows(me)]
            for d in hops:
                cs_copy(it, q, d).wait_recv()
                total = total + cr[it, q, d - 1]
            ca[it, q] = total
            for d in hops:
                ca_copy(it, q, d).start()
            cq[it, q, own_rows(me)] = total
        if with_v:
            total = v[rows(q), my_cols]
            for d in hops:
                rs_copy(k, q, d).wait_recv()
                total = total + gr[k, q, d - 1].astype(F32)
            ag[k, q] = total.astype(BF16)
            for d in hops:
                ag_copy(k, q, d).start()
            aq[k, q, :, my_cols] = total.astype(BF16)

    def ag_wait(k, q, with_v, it):
        if it is not None:
            for d in hops:
                ca_arrive(it, q, d).wait_recv()
        if with_v:
            for d in hops:
                ag_arrive(k, q, d).wait_recv()

    def gamma_wait(it, q):
        total = gm[it, q]
        for d in range(1, src_size):
            gm_copy(it, q, d).wait_recv()
            total = total + gmr[it, q, d - 1]
        coef[0, it, q] = total
        if it > 0:
            coef[1, it, q] = total / coef[0, it - 1, q]

    def alpha_of(it, q):
        return coef[0, it, q] / cq[it, q]

    def close(it, q):
        a = alpha_of(it, q)
        coef[2, it, q] = a
        r = rows(q)
        if it == 0:
            dirn[r, :] = grad[r, :]
            slip_ref[r, :] = a[:, :1] * grad[r, :]
        else:
            d = grad[r, :] + coef[1, it, q][:, :1] * dirn[r, :]
            dirn[r, :] = d
            slip_ref[r, :] = slip_ref[r, :] + a[:, :1] * d

    def open_grad(it, q):
        r = rows(q)
        ps = ps_ref[...].astype(F32)
        full = aq[it, q].astype(F32)
        if it == 0:
            g = ps * full
        else:
            prev = it - 1
            if prev == 0:
                q_dir = full
            else:
                q_dir = full + coef[1, prev, q][:, :1] * vdir[r, :]
            vdir[r, :] = q_dir
            g = grad[r, :] - coef[2, prev, q][:, :1] * (ps * q_dir)
        grad[r, :] = g
        gbf[r, :] = g.astype(BF16)
        gm[it, q] = jnp.broadcast_to(jnp.sum(g * g, axis=1, keepdims=True), (eg, LANES))
        for d in range(1, src_size):
            gm_copy(it, q, d).start()

    def f1(it, q, begin, end):
        def step(c, _):
            @pl.when(c < chunks)
            def _():
                for i in range(gpc):
                    g = c * gpc + i
                    part[it, g, rows(q), :] = lax.dot_general(
                        gbf[rows(q), :], green[g], (((1,), (1,)), ((), ())),
                        preferred_element_type=F32).astype(BF16)
                s1_copy(it, q, c).start()

            @pl.when(c >= LAG)
            def _():
                b = c - LAG
                s1_copy(it, q, b).wait_recv()
                xs[it, span(b), packed(q)] = (
                    part[it, span(b), mine(q)].astype(F32)
                    + r1[it, span(b), packed(q)].astype(F32)).astype(BF16)
                x_copy(it, q, b).start()
            return 0

        lax.fori_loop(begin, end, step, 0)

    def f2(it, q, begin, end):
        def step(c, _):
            @pl.when(c < chunks)
            def _():
                x_copy(it, q, c).wait_recv()
                for i in range(gpc):
                    g = c * gpc + i
                    w = wg_ref[g].astype(F32)
                    u[it, g, mine(q), :] = (w * (
                        xs[it, g, packed(q)].astype(F32)
                        + xr[it, g, packed(q)].astype(F32))).astype(BF16)
                u_copy(it, q, c).start()

            @pl.when(c >= LAG)
            def _():
                b = c - LAG
                u_arrive(it, q, b).wait_recv()
                for i in range(gpc):
                    g = b * gpc + i
                    ug = u[it, g, rows(q), :]
                    if it + 1 < ITERS:
                        v[rows(q), :] += jnp.dot(ug, green[g], preferred_element_type=F32)
                    p = u[0, g, rows(q), :].astype(F32)
                    for k in range(1, it + 1):
                        p = u[k, g, rows(q), :].astype(F32) + coef[1, k, q][:, :1] * p
                    p = p * p
                    acc = csum[it, q]
                    for t in range(times // LANES):
                        acc = acc + p[:, t * LANES:(t + 1) * LANES]
                    csum[it, q] = acc
            return 0

        lax.fori_loop(begin, end, step, 0)

    v[...] = jnp.zeros_like(v)
    csum[...] = jnp.zeros_like(csum)

    def first(g, _):
        w = wg_ref[g].astype(F32)
        r0 = (w * obs_ref[:, g, :]).astype(BF16)
        green_copy(g).wait()
        v[...] += jnp.dot(r0, green[g], preferred_element_type=F32)
        return 0

    lax.fori_loop(0, gauges, first, 0)

    for q in range(GROUPS):
        rs_start(0, q, True, None)
    ag_start(0, 0, True, None)

    mid = chunks // 2
    last = chunks + LAG
    for it in range(ITERS):
        prev = it - 1 if it > 0 else None
        for q in range(GROUPS):
            ag_wait(it, q, True, prev)
            if prev is not None:
                close(prev, q)
            open_grad(it, q)
            if q + 1 < GROUPS:
                f1(it, q, 0, mid)
                ag_start(it, q + 1, True, prev)
                f1(it, q, mid, last)
            else:
                f1(it, q, 0, last)
        with_v = it + 1 < ITERS
        v[...] = jnp.zeros_like(v)
        for q in range(GROUPS):
            gamma_wait(it, q)
            if q > 0:
                f2(it, q, 0, mid)
                ag_start(it + 1, q - 1, with_v, it)
                f2(it, q, mid, last)
            else:
                f2(it, q, 0, last)
            rs_start(it + 1, q, with_v, it)
    ag_start(ITERS, GROUPS - 1, False, ITERS - 1)
    weights = []
    for q in range(GROUPS):
        ag_wait(ITERS, q, False, ITERS - 1)
        close(ITERS - 1, q)
        total = coef[2, ITERS - 1, q]
        ws = [total]
        for k in range(ITERS - 2, -1, -1):
            total = coef[2, k, q] + coef[1, k + 1, q] * total
            ws.insert(0, total)
        for k in range(ITERS):
            coef[0, k, q] = ws[k]

    def finish(g, _):
        w = wg_ref[g].astype(F32)
        for q in range(GROUPS):
            out = w * obs_ref[rows(q), g, :]
            for k in range(ITERS):
                out = out - coef[0, k, q][:, :1] * u[k, g, rows(q), :].astype(F32)
            res_ref[rows(q), g, :] = out
        return 0

    lax.fori_loop(0, gauges, finish, 0)

    def drain(c, _):
        for it in range(ITERS):
            for q in range(GROUPS):
                s1_copy(it, q, c).wait_send()
                x_copy(it, q, c).wait_send()
                u_copy(it, q, c).wait_send()
        return 0

    lax.fori_loop(0, chunks, drain, 0)
    for it in range(ITERS):
        for q in range(GROUPS):
            for d in hops:
                rs_copy(it, q, d).wait_send()
                ag_copy(it, q, d).wait_send()
                cs_copy(it, q, d).wait_send()
                ca_copy(it, q, d).wait_send()
            for d in range(1, src_size):
                gm_copy(it, q, d).wait_send()


def fused(peers, src_size, green, observed, gauge_mask, source_mask):
    gauges, times, width = green.shape
    events = observed.shape[0]
    eg = events // GROUPS
    own = eg // peers
    gpc = 2
    chunks = gauges // gpc
    vm = pltpu.VMEM
    dma = pltpu.SemaphoreType.DMA
    n = peers - 1
    m = src_size - 1
    scratch = [
        vm((gauges, times, width), BF16),
        vm((ITERS, gauges, events, times), BF16),
        vm((ITERS, gauges, events // 2, times), BF16),
        vm((ITERS, gauges, events // 2, times), BF16),
        vm((ITERS, gauges, events // 2, times), BF16),
        vm((ITERS, gauges, events, times), BF16),
        vm((events, width), F32),
        vm((events, width), F32),
        vm((events, width), BF16),
        vm((events, width), F32),
        vm((events, width), F32),
        vm((ITERS, GROUPS, eg, LANES), F32),
        vm((3, ITERS, GROUPS, eg, LANES), F32),
        vm((ITERS, GROUPS, eg, width), BF16),
        vm((ITERS, GROUPS, n, eg, LANES), BF16),
        vm((ITERS, GROUPS, eg, LANES), BF16),
        vm((ITERS, GROUPS, eg, width), BF16),
        vm((ITERS, GROUPS, n, own, LANES), F32),
        vm((ITERS, GROUPS, own, LANES), F32),
        vm((ITERS, GROUPS, eg, LANES), F32),
        vm((ITERS, GROUPS, eg, LANES), F32),
        vm((ITERS, GROUPS, m, eg, LANES), F32),
        dma((gauges,)),
    ] + [dma((ITERS, GROUPS, chunks))] * 6 + [dma((ITERS, GROUPS, n))] * 8 + [dma((ITERS, GROUPS, m))] * 2
    slip, res = pl.pallas_call(
        functools.partial(cg_kernel, peers, src_size, gpc),
        out_shape=(
            jax.ShapeDtypeStruct((events, width), F32),
            jax.ShapeDtypeStruct((events, gauges, times), F32),
        ),
        in_specs=[
            pl.BlockSpec(memory_space=pl.ANY),
            pl.BlockSpec(memory_space=pltpu.VMEM),
            pl.BlockSpec(memory_space=pltpu.SMEM),
            pl.BlockSpec(memory_space=pltpu.VMEM),
        ],
        out_specs=[pl.BlockSpec(memory_space=pltpu.VMEM)] * 2,
        scratch_shapes=scratch,
        compiler_params=pltpu.CompilerParams(
            collective_id=0, has_side_effects=True, vmem_limit_bytes=67043328),
    )(green, observed, gauge_mask, source_mask.reshape(1, width))
    return slip, res


def project(vector, green):
    return lax.dot_general(
        vector, green, (((1,), (2,)), ((), ())), preferred_element_type=F32)


def gradient(green, wave, ps_local):
    part = lax.dot_general(
        wave.astype(BF16), green, (((1, 2), (0, 1)), ((), ())), preferred_element_type=F32)
    grad = ps_local * lax.psum(part.astype(BF16), "gauge").astype(F32)
    gamma = lax.psum(jnp.sum(grad * grad, axis=1), "src")
    return (grad, gamma)


def general(green, observed, gauge_mask, source_mask):
    wg = gauge_mask.astype(F32)[None, :, None]
    ps_local = source_mask.astype(F32)[None, :]
    residual = wg * observed
    events = observed.shape[0]
    slip = jnp.zeros((events, green.shape[2]), F32)
    grad, gamma = gradient(green, residual, ps_local)
    direction = grad
    for step in range(ITERS):
        rows = events // lax.axis_size("src")
        offset = lax.axis_index("src") * rows
        predicted = wg * lax.psum_scatter(
            project(direction.astype(BF16), green).astype(BF16),
            "src", scatter_dimension=0, tiled=True).astype(F32)
        curvature = lax.psum(jnp.sum(predicted * predicted, axis=(1, 2)), "gauge")
        alpha_rows = lax.dynamic_slice_in_dim(gamma, offset, rows, 0) / curvature
        kept = (lax.dynamic_slice_in_dim(residual, offset, rows, 0)
                - alpha_rows[:, None, None] * predicted)
        residual = lax.all_gather(kept.astype(BF16), "src", axis=0, tiled=True).astype(F32)
        alpha = lax.all_gather(alpha_rows.astype(BF16), "src", axis=0, tiled=True).astype(F32)
        slip = slip + alpha[:, None] * direction
        if step + 1 < ITERS:
            grad, fresh = gradient(green, residual, ps_local)
            direction = grad + (fresh / gamma)[:, None] * direction
            gamma = fresh
    return (slip, residual)


def per_device(peers, src_size, green, observed, gauge_mask, source_mask):
    events, gauges, times = observed.shape
    fits = (
        src_size == 2 * PAIR
        and green.shape[2] == peers * LANES
        and gauges % 4 == 0
        and gauges % 8 == 0
        and events % (GROUPS * 8 * peers) == 0
        and events % (GROUPS * 32) == 0
        and times % LANES == 0
    )
    if fits:
        return fused(peers, src_size, green, observed, gauge_mask, source_mask)
    return general(green, observed, gauge_mask, source_mask)


def solution(mesh):
    return jax.shard_map(
        functools.partial(per_device, mesh.shape["gauge"], mesh.shape["src"]),
        mesh=mesh,
        in_specs=(P("gauge", None, "src"), P(None, "gauge", None), P("gauge"), P("src")),
        out_specs=(P(None, "src"), P(None, "gauge", None)),
        check_vma=False,
    )
```

time: 549 us -> 152 us (0.28)
  waiting for transfers between devices: 350 us -> 0 us
  Pallas kernels: 0 us -> 144 us
  blocking collectives: 87.3 us -> 0 us
  matrix products: 66.6 us -> 0 us
  other arithmetic: 20.9 us -> 0 us
  between operations: 14.6 us -> 0.64 us
    psum x3 -> x0, waiting for transfers between devices: 216 us -> none  [gradient(): lax.psum(part.astype(jnp.bfloat16), 'gauge').astype(jnp.float32)]
    pallas_call x0 -> x1, Pallas kernels: none -> 144 us  [fused(): pl.pallas_call(functools.partial(cg_kernel, peers, src_size, gpc), out_sh...]
    reduce_scatter x3 -> x0, waiting for transfers between devices: 86.1 us -> none  [per_device(): lax.psum_scatter(project(direction_bf, green).astype(jnp.bfloat16), 'src'...]
    psum x6 -> x0, blocking collectives: 81.3 us -> none  [the longest x3 64.1 us: per_device(): curvature = lax.psum(jnp.sum(predicted * predicted, axis=(1, 2)), 'gauge')]
    dot_general x6 -> x0, matrix products: 66.6 us -> none  [the longest x3 38.7 us: project(): lax.dot_general(vector, green, (((1,), (2,)), ((), ())), preferred_elemen...]
    all_gather x3 -> x0, waiting for transfers between devices: 47.8 us -> none  [per_device(): lax.all_gather(kept.astype(jnp.bfloat16), 'src', axis=0, tiled=True)]
    convert_element_type x11 -> x0, other arithmetic: 8.71 us -> none  [the longest x3 7.8 us: per_device(): kept.astype(jnp.bfloat16)]
    reduce_sum x6 -> x0, other arithmetic: 6.4 us -> none  [the longest x3 4.05 us: per_device(): curvature = lax.psum(jnp.sum(predicted * predicted, axis=(1, 2)), 'gauge')]
  transfers between devices with their start and end apart: 9 -> 0, of which waited for: 9 -> 0; matrix products, arithmetic and copies ran while one was open for 0% -> 0% of each run, Pallas kernels for 0% -> 0%
where the time goes in v1:
time: 152 us
  Pallas kernels  144 us (95%)
  local copies, waits for them, and re-layouts  6.92 us (5%)
    pallas_call x1, Pallas kernels, fused(): pl.pallas_call(functools.partial(cg_kernel, peers, src_size, gpc), out_sh...  144 us
    unnamed x2, local copies, waits for them, and re-layouts  6.92 us

profile of v1, /device:TPU:0, one launch (start us, length us, event | category | flops | bytes accessed | tf_op | source)
XLA Modules:
  0.0 151.6 jit_solution(8229594804974866988)
XLA Ops:
  0.6 144.1 %shard_map.59 = (f32[128,1024]{1,0:T(8,128)}, f32[128,16,512]{2,1,0:T(8,128)}) custom-call(bf16[16,512,1024]{2,1,0:T(8,128)(2,1)} %green_hbm.1, f32[128,16,512]{2,1,0:T(8,128)} %obs_ref.1, s32[16]{0:T(128)} %wg_ref.1, s32[1,1024]{1,0:T(1,128)} %bitcast.1), custom_call_target="tpu_custom_call" | custom-call | tf_op jit(solution)/shard_map/pallas_call | solution.py:402
  144.7 1.9 %copy.8 = f32[128,1024]{1,0:T(8,128)} copy(f32[128,1024]{1,0:T(8,128)} %get-tuple-element.4) | data formatting | bytes 1048576
  146.6 5.0 %copy.9 = f32[128,16,512]{2,1,0:T(8,128)} copy(f32[128,16,512]{2,1,0:T(8,128)} %get-tuple-element.5) | data formatting | bytes 8388608
